TPU v7x, 32 devices: a whole 2x2x4 slice. The times are simulated.
32 devices in a mesh: dp: 8 (over y, x, core), tensor: 4 (over z).
Axes of the slice: x: 2, y: 2, z: 4, core: 2. Of those that a mesh axis runs over, the one named last changes fastest.
Arguments:
- saved_input: bfloat16 [2048, 6144], P('dp', 'tensor'), may hold values from -6 to 6
- queries: bfloat16 [2048, 1024], P('dp', 'tensor'), may hold values from -8 to 8
- keys: bfloat16 [2048, 1024], P('dp', 'tensor'), may hold values from -8 to 8
- value_weight: bfloat16 [6144, 1024], P(None, 'tensor'), may hold values from -0.109375 to 0.109375
- grad_attended: bfloat16 [2048, 1024], P('dp', 'tensor'), may hold values from -6 to 6
Outputs:
- grad_input: bfloat16 [2048, 6144], P('dp', 'tensor')
- grad_value_weight: float32 [6144, 1024], P('dp', 'tensor')
- grad_queries: bfloat16 [2048, 1024], P('dp', 'tensor')
- grad_keys: bfloat16 [2048, 1024], P('dp', 'tensor')
All inputs are finite; a program needn't handle non-finite values.
Results may differ from a plain program's by a relative error of at most 0.02.
Values may be sent and summed in bfloat16 or wider, within the bound.
A program may use at most 64 MiB of HBM per device.

v0:
```python
import jax
import jax.numpy as jnp
from jax import lax
from jax.sharding import PartitionSpec as P

HD = 128


def on_device(saved_input, queries, keys, value_weight, grad_attended):
    token_count = queries.shape[0]
    local_width = value_weight.shape[1]
    local_heads = local_width // HD
    score_scale = 1.0 / jnp.sqrt(jnp.float32(HD))
    full_input = lax.all_gather(saved_input, "tensor", axis=1, tiled=True)
    values = jnp.dot(full_input, value_weight, preferred_element_type=jnp.float32).astype(
        jnp.bfloat16
    )
    query_heads = queries.reshape(token_count, local_heads, HD)
    key_heads = keys.reshape(token_count, local_heads, HD)
    value_heads = values.reshape(token_count, local_heads, HD)
    grad_heads = grad_attended.reshape(token_count, local_heads, HD)
    scores = (
        jnp.einsum("qhd,khd->hqk", query_heads, key_heads, preferred_element_type=jnp.float32)
        * score_scale
    )
    positions = lax.iota(jnp.int32, token_count)
    causal = positions[:, None] >= positions[None, :]
    scores = jnp.where(causal[None], scores, -jnp.inf)
    row_max = jnp.max(scores, axis=-1, keepdims=True)
    weights_exp = jnp.exp(scores - row_max)
    attention = weights_exp / jnp.sum(weights_exp, axis=-1, keepdims=True)
    probs_half = attention.astype(jnp.bfloat16)
    grad_values = jnp.einsum(
        "hqk,qhd->khd", probs_half, grad_heads, preferred_element_type=jnp.float32
    ).astype(jnp.bfloat16)
    grad_probs = jnp.einsum(
        "qhd,khd->hqk", grad_heads, value_heads, preferred_element_type=jnp.float32
    )
    row_dot = jnp.sum(attention * grad_probs, axis=-1, keepdims=True)
    grad_scores = (attention * (grad_probs - row_dot) * score_scale).astype(jnp.bfloat16)
    grad_queries = jnp.einsum(
        "hqk,khd->qhd", grad_scores, key_heads, preferred_element_type=jnp.float32
    ).astype(jnp.bfloat16)
    grad_keys = jnp.einsum(
        "hqk,qhd->khd", grad_scores, query_heads, preferred_element_type=jnp.float32
    ).astype(jnp.bfloat16)
    value_flat = grad_values.reshape(token_count, local_width)
    data_groups = lax.axis_size("dp")
    partial_value = lax.dot_general(
        value_flat, value_weight, (((1,), (1,)), ((), ())), preferred_element_type=jnp.float32
    )
    grad_input = lax.psum_scatter(
        partial_value.astype(jnp.bfloat16), "tensor", scatter_dimension=1, tiled=True
    )
    partial_value = lax.dot_general(
        full_input, value_flat, (((0,), (0,)), ((), ())), preferred_element_type=jnp.float32
    )
    summed = lax.psum_scatter(
        partial_value.astype(jnp.bfloat16), "dp", scatter_dimension=0, tiled=True
    ).astype(jnp.float32)
    grad_value_weight = summed / jnp.float32(data_groups)
    return (
        grad_input,
        grad_value_weight,
        grad_queries.reshape(token_count, local_width),
        grad_keys.reshape(token_count, local_width),
    )


def solution(mesh):
    placed = (
        P("dp", "tensor"),
        P("dp", "tensor"),
        P("dp", "tensor"),
        P(None, "tensor"),
        P("dp", "tensor"),
    )
    return jax.shard_map(
        on_device,
        mesh=mesh,
        in_specs=placed,
        out_specs=(P("dp", "tensor"), P("dp", "tensor"), P("dp", "tensor"), P("dp", "tensor")),
        check_vma=False,
    )
```

profile of v0, /device:TPU:0, one launch (start us, length us, event | category | flops | bytes accessed | tf_op | source)
XLA Modules:
  0.0 195.0 jit_solution(18344579385633237910)
XLA Ops:
  7.2 0.0 copy-start
  7.2 0.0 all-gather.2.cloned.1.call-start
  7.2 0.7 all-gather.2.cloned.1.call-update
  7.9 0.0 reduce-scatter.5.cloned.1.call-start
  8.0 1.2 copy.26
  9.1 1.0 copy.27
  10.2 1.2 fusion.28
  11.3 1.5 convolution_convert_fusion.4
  12.9 62.9 %all-gather.2.cloned.1.call-done = bf16[256,6144]{1,0:T(8,128)(2,1)} async-done(((bf16[256,1536]{1,0:T(8,128)(2,1)}), bf16[256,6144]{1,0:T(8,128)(2,1)}) %all-gather.2.cloned.1.call-update) | async-done | bytes 3145744 | tf_op jit(solution)/shard_map/all_gather | solution.py:14
  75.8 4.6 %fusion.2 = bf16[6144,256]{0,1:T(8,128)(2,1)} fusion(bf16[256,256]{0,1:T(8,128)(2,1)S(1)} %bitcast.41, bf16[256,6144]{1,0:T(8,128)(2,1)} %all-gather.2.cloned.1.call-done), kind=kOutput, calls=%fused_computation.4 | convolution fusion | flops 806879232 | bytes 6422528 | tf_op jit(solution)/shard_map/dot_general | solution.py:55
  80.3 0.0 reduce-scatter.5.cloned.1.call-update
  80.4 0.0 reduce-scatter.3.cloned.1.call-start
  80.4 2.7 %convolution_convert_fusion.1 = bf16[256,6144]{1,0:T(8,128)(2,1)} fusion(bf16[256,256]{0,1:T(8,128)(2,1)S(1)} %bitcast.42, bf16[6144,256]{1,0:T(8,128)(2,1)S(1)} %copy-done), kind=kOutput, calls=%fused_computation.3 | convolution fusion | flops 806879232 | bytes 6422528 | tf_op jit(solution)/shard_map/dot_general | solution.py:49
  83.1 0.0 reduce-scatter.3.cloned.1.call-update
  83.2 3.5 %convolution_convert_fusion.5 = bf16[256,256]{0,1:T(8,128)(2,1)S(1)} fusion(bf16[256,6144]{1,0:T(8,128)(2,1)} %all-gather.2.cloned.1.call-done, bf16[6144,256]{1,0:T(8,128)(2,1)S(1)} %copy-done), kind=kOutput, calls=%fused_computation.17 | convolution fusion | flops 805371904 | bytes 6422528 | tf_op jit(solution)/shard_map/dot_general | solution.py:15
  86.7 1.1 convolution_bitcast_fusion
  87.8 2.0 %convolution_convert_fusion.2 = bf16[2,256,128]{1,2,0:T(8,128)(2,1)S(1)} fusion(bf16[256,2,128]{0,2,1:T(8,128)(2,1)S(1)} %bitcast.49, f32[2,256,256]{1,2,0:T(8,128)} %convolution_bitcast_fusion, f32[2,256,256]{1,2,0:T(8,128)} %get-tuple-element.9, f32[2,256]{1,0:T(2,128)S(1)} %get-tuple-element.8), kind=kOutput, calls=%fused_computation.14 | convolution fusion | flops 34538240 | bytes 1312768 | tf_op jit(solution)/shard_map/hqk,khd->qhd/dot_general | solution.py:41
  89.7 0.8 copy.20
  90.5 2.0 %convolution_convert_fusion.3 = bf16[2,256,128]{1,2,0:T(8,128)(2,1)S(1)} fusion(bf16[256,2,128]{0,2,1:T(8,128)(2,1)S(1)} %bitcast.46, f32[2,256,256]{1,2,0:T(8,128)} %convolution_bitcast_fusion, f32[2,256,256]{1,2,0:T(8,128)} %get-tuple-element.9, f32[2,256]{1,0:T(2,128)S(1)} %get-tuple-element.8), kind=kOutput, calls=%fused_computation.15 | convolution fusion | flops 34538240 | bytes 1312768 | tf_op jit(solution)/shard_map/hqk,qhd->khd/dot_general | solution.py:44
  92.5 0.8 copy.21
  93.2 32.0 %reduce-scatter.5.cloned.1.call-done = bf16[768,256]{0,1:T(8,128)(2,1)} async-done(((bf16[6144,256]{0,1:T(8,128)(2,1)}), bf16[768,256]{0,1:T(8,128)(2,1)}) %reduce-scatter.5.cloned.1.call-update) | async-done | bytes 393232 | tf_op jit(solution)/shard_map/reduce_scatter | solution.py:58
  125.2 1.9 convert_multiply_fusion
  127.1 2.3 %copy.19 = f32[768,256]{1,0:T(8,128)} copy(f32[768,256]{0,1:T(8,128)} %convert_multiply_fusion) | data formatting | bytes 1572864
  129.4 59.1 %reduce-scatter.3.cloned.1.call-done = bf16[256,1536]{1,0:T(8,128)(2,1)} async-done(((bf16[256,6144]{1,0:T(8,128)(2,1)}), bf16[256,1536]{1,0:T(8,128)(2,1)}) %reduce-scatter.3.cloned.1.call-update) | async-done | bytes 786448 | tf_op jit(solution)/shard_map/reduce_scatter | solution.py:52
  (6 shorter events, 0.0 us)
Async XLA Ops:
  7.2 73.2 %copy-start = (bf16[6144,256]{1,0:T(8,128)(2,1)S(1)}, bf16[6144,256]{1,0:T(8,128)(2,1)}, u32[]{:S(2)}) copy-start(bf16[6144,256]{1,0:T(8,128)(2,1)} %param.8) | copy-start | bytes 9437188
  7.2 68.6 %all-gather.2.cloned.1.call-start = ((), (), s32[]{:S(2)}) async-start(), calls=%async_computation.3 | async-start | bytes 3932160 | tf_op jit(solution)/shard_map/all_gather | solution.py:14
  7.9 117.3 %reduce-scatter.5.cloned.1.call-start = ((), (), s32[]{:S(2)}) async-start(), calls=%async_computation.4 | async-start | bytes 3538944 | tf_op jit(solution)/shard_map/reduce_scatter | solution.py:58
  10.2 1.2 copy-start.2
  80.4 108.1 %reduce-scatter.3.cloned.1.call-start = ((), (), s32[]{:S(2)}) async-start(), calls=%async_computation.2 | async-start | bytes 3932160 | tf_op jit(solution)/shard_map/reduce_scatter | solution.py:52
  83.2 3.5 %copy-start.1 = (bf16[256,256]{1,0:T(8,128)(2,1)S(1)}, bf16[256,256]{1,0:T(8,128)(2,1)}, u32[]{:S(2)}) copy-start(bf16[256,256]{1,0:T(8,128)(2,1)} %param.9) | copy-start | bytes 393220
Sparse Core Ops, SparseCore 0:
  9.6 66.1 all-gather.1
  80.5 44.6 reduce-scatter.4
  128.1 60.3 reduce-scatter.2
where the time goes:
time: 195 us
  waiting for transfers between devices  155 us (79%)
  matrix products  18.5 us (9%)
  between operations  13.8 us (7%)
  local copies, waits for them, and re-layouts  5.98 us (3%)
  other arithmetic  1.95 us (1%)
    all_gather x1, waiting for transfers between devices, on_device(): full_input = lax.all_gather(saved_input, 'tensor', axis=1, tiled=True)  62.9 us
    reduce_scatter x1, waiting for transfers between devices, on_device(): lax.psum_scatter(partial_value.astype(jnp.bfloat16), 'tensor', scatter_di...  59.1 us
    reduce_scatter x1, waiting for transfers between devices, on_device(): lax.psum_scatter(partial_value.astype(jnp.bfloat16), 'dp', scatter_dimens...  32 us
    dot_general x1, matrix products, on_device(): lax.dot_general(full_input, value_flat, (((0,), (0,)), ((), ())), preferr...  4.58 us
  transfers between devices with their start and end apart: 3, of which 3 were waited for; matrix products, arithmetic and copies ran while one was open for 11% of the time, Pallas kernels for 0%

commit v1 on v0

--- a/solution.py
+++ b/solution.py
@@ -11,7 +11,8 @@
     local_width = value_weight.shape[1]
     local_heads = local_width // HD
     score_scale = 1.0 / jnp.sqrt(jnp.float32(HD))
-    full_input = lax.all_gather(saved_input, "tensor", axis=1, tiled=True)
+    blocks = lax.all_gather(saved_input, "tensor", axis=0, tiled=False)
+    full_input = jnp.concatenate(blocks, axis=1)
     values = jnp.dot(full_input, value_weight, preferred_element_type=jnp.float32).astype(
         jnp.bfloat16
     )

time: 195 us -> 200 us (1.026)
  local copies, waits for them, and re-layouts: 5.98 us -> 10.7 us
    reshape x0 -> x1, local copies, waits for them, and re-layouts: none -> 4.73 us  [on_device(): full_input = jnp.concatenate(blocks, axis=1)]
where the time goes in v1:
time: 200 us
  waiting for transfers between devices  155 us (78%)
  matrix products  18.5 us (9%)
  between operations  13.8 us (7%)
  local copies, waits for them, and re-layouts  10.7 us (5%)
    all_gather x1, waiting for transfers between devices, on_device(): blocks = lax.all_gather(saved_input, 'tensor', axis=0, tiled=False)  62.9 us
    reduce_scatter x1, waiting for transfers between devices, on_device(): lax.psum_scatter(partial_value.astype(jnp.bfloat16), 'tensor', scatter_di...  59.1 us
    reduce_scatter x1, waiting for transfers between devices, on_device(): lax.psum_scatter(partial_value.astype(jnp.bfloat16), 'dp', scatter_dimens...  32 us
    reshape x1, local copies, waits for them, and re-layouts, on_device(): full_input = jnp.concatenate(blocks, axis=1)  4.73 us
    dot_general x1, matrix products, on_device(): lax.dot_general(full_input, value_flat, (((0,), (0,)), ((), ())), preferr...  4.61 us
  transfers between devices with their start and end apart: 3, of which 3 were waited for; matrix products, arithmetic and copies ran while one was open for 11% of the time, Pallas kernels for 0%

profile of v1, /device:TPU:0, one launch (start us, length us, event | category | flops | bytes accessed | tf_op | source)
XLA Modules:
  0.0 199.8 jit_solution(5724853048283546005)
XLA Ops:
  7.2 0.0 all-gather.3.cloned.1.call-start
  7.2 0.7 all-gather.3.cloned.1.call-update
  7.9 0.0 reduce-scatter.5.cloned.1.call-start
  8.0 1.2 copy.53
  9.1 1.0 copy.54
  10.2 1.2 fusion.28
  11.3 1.5 convolution_convert_fusion.4
  12.9 62.9 %all-gather.3.cloned.1.call-done = bf16[1024,1536]{1,0:T(8,128)(2,1)} async-done(((bf16[256,1536]{1,0:T(8,128)(2,1)}), bf16[1024,1536]{1,0:T(8,128)(2,1)}) %all-gather.3.cloned.1.call-update) | async-done | bytes 3145744 | tf_op jit(solution)/shard_map/all_gather | solution.py:14
  75.8 4.7 %copy.39 = bf16[256,4,1536]{0,2,1:T(8,128)(2,1)} copy(bf16[256,4,1536]{2,0,1:T(8,128)(2,1)} %bitcast.47) | data formatting | bytes 6291456 | tf_op jit(solution)/shard_map/reshape | solution.py:15
  80.5 4.6 %fusion.2 = bf16[6144,256]{0,1:T(8,128)(2,1)} fusion(bf16[256,256]{0,1:T(8,128)(2,1)S(1)} %bitcast.48, bf16[256,6144]{0,1:T(8,128)(2,1)} %bitcast.45), kind=kOutput, calls=%fused_computation.4 | convolution fusion | flops 806879232 | bytes 6422528 | tf_op jit(solution)/shard_map/dot_general | solution.py:56
  85.1 0.0 reduce-scatter.5.cloned.1.call-update
  85.1 0.0 reduce-scatter.3.cloned.1.call-start
  85.2 2.7 %convolution_convert_fusion.1 = bf16[256,6144]{1,0:T(8,128)(2,1)} fusion(bf16[256,256]{0,1:T(8,128)(2,1)S(1)} %bitcast.49, bf16[6144,256]{1,0:T(8,128)(2,1)S(1)} %copy-done), kind=kOutput, calls=%fused_computation.3 | convolution fusion | flops 806879232 | bytes 6422528 | tf_op jit(solution)/shard_map/dot_general | solution.py:50
  87.9 0.0 reduce-scatter.3.cloned.1.call-update
  87.9 3.5 %convolution_convert_fusion.5 = bf16[256,256]{0,1:T(8,128)(2,1)S(1)} fusion(bf16[256,6144]{0,1:T(8,128)(2,1)} %bitcast.46, bf16[6144,256]{1,0:T(8,128)(2,1)S(1)} %copy-done), kind=kOutput, calls=%fused_computation.17 | convolution fusion | flops 805371904 | bytes 6422528 | tf_op jit(solution)/shard_map/dot_general | solution.py:16
  91.5 1.1 convolution_bitcast_fusion
  92.5 2.0 convolution_convert_fusion.2
  94.5 0.8 copy.47
  95.3 2.0 convolution_convert_fusion.3
  97.2 0.8 copy.48
  98.0 32.0 %reduce-scatter.5.cloned.1.call-done = bf16[768,256]{0,1:T(8,128)(2,1)} async-done(((bf16[6144,256]{0,1:T(8,128)(2,1)}), bf16[768,256]{0,1:T(8,128)(2,1)}) %reduce-scatter.5.cloned.1.call-update) | async-done | bytes 393232 | tf_op jit(solution)/shard_map/reduce_scatter | solution.py:59
  129.9 1.9 convert_multiply_fusion
  131.9 2.3 %copy.46 = f32[768,256]{1,0:T(8,128)} copy(f32[768,256]{0,1:T(8,128)} %convert_multiply_fusion) | data formatting | bytes 1572864
  134.2 59.1 %reduce-scatter.3.cloned.1.call-done = bf16[256,1536]{1,0:T(8,128)(2,1)} async-done(((bf16[256,6144]{1,0:T(8,128)(2,1)}), bf16[256,1536]{1,0:T(8,128)(2,1)}) %reduce-scatter.3.cloned.1.call-update) | async-done | bytes 786448 | tf_op jit(solution)/shard_map/reduce_scatter | solution.py:53
  (7 shorter events, 0.0 us)
Async XLA Ops:
  7.2 78.0 %copy-start = (bf16[6144,256]{1,0:T(8,128)(2,1)S(1)}, bf16[6144,256]{1,0:T(8,128)(2,1)}, u32[]{:S(2)}) copy-start(bf16[6144,256]{1,0:T(8,128)(2,1)} %param.8) | copy-start | bytes 9437188
  7.2 68.6 %all-gather.3.cloned.1.call-start = ((), (), s32[]{:S(2)}) async-start(), calls=%async_computation.4 | async-start | bytes 3932160 | tf_op jit(solution)/shard_map/all_gather | solution.py:14
  7.9 122.0 %reduce-scatter.5.cloned.1.call-start = ((), (), s32[]{:S(2)}) async-start(), calls=%async_computation.3 | async-start | bytes 3538944 | tf_op jit(solution)/shard_map/reduce_scatter | solution.py:59
  10.2 1.2 copy-start.2
  85.1 108.1 %reduce-scatter.3.cloned.1.call-start = ((), (), s32[]{:S(2)}) async-start(), calls=%async_computation.2 | async-start | bytes 3932160 | tf_op jit(solution)/shard_map/reduce_scatter | solution.py:53
  87.9 3.5 %copy-start.1 = (bf16[256,256]{1,0:T(8,128)(2,1)S(1)}, bf16[256,256]{1,0:T(8,128)(2,1)}, u32[]{:S(2)}) copy-start(bf16[256,256]{1,0:T(8,128)(2,1)} %param.9) | copy-start | bytes 393220
Sparse Core Ops, SparseCore 0:
  9.6 66.1 all-gather.2
  85.2 44.6 reduce-scatter.4
  132.8 60.3 reduce-scatter.2
